TPU v7x, 32 devices: a whole 2x2x4 slice. The times are simulated.
32 devices in a mesh: pipe: 4 (over y, core), vocab: 2 (over x), expert: 4 (over z).
Axes of the slice: x: 2, y: 2, z: 4, core: 2. Of those that a mesh axis runs over, the one named last changes fastest.
Arguments:
- token_ids: int32 [192], replicated, may hold values from 0 to 65535
- routes: int32 [192, 2], replicated, may hold values from 0 to 3, all different within a row; in each aligned block of 192 rows (0 to 191, 192 to 383, ...) at most 144 rows name the same one
- gate_weights: float32 [192, 2], replicated, may hold values from 0.2 to 1
- embed_table: bfloat16 [65536, 7168], P(('pipe', 'vocab'), 'expert'), may hold values from -0.59765625 to 0.59765625
- w_gate: bfloat16 [4, 7168, 2048], P('expert', None, ('pipe', 'vocab')), may hold values from -0.5 to 0.5
- w_up: bfloat16 [4, 7168, 2048], P('expert', None, ('pipe', 'vocab')), may hold values from -0.5 to 0.5
- w_down: bfloat16 [4, 2048, 7168], P('expert', ('pipe', 'vocab')), may hold values from -0.125 to 0.125
Outputs:
- logits: bfloat16 [192, 65536], P('expert', ('pipe', 'vocab'))
Inputs may be any that keep to these rules, and one draw needn't show every extreme that they name: `routes`: each row names 2 different experts; over all 192 rows no expert is named more than 144 times, a bound that some block reaches.
All inputs are finite; a program needn't handle non-finite values.
Results may differ from a plain program's by a relative error of at most 0.025.
Values may be sent and summed in bfloat16 or wider, within the bound.
A program may use at most 128 MiB of HBM per device.

v0:
```python
import jax
import jax.numpy as jnp
from jax import lax
from jax.sharding import PartitionSpec as P


def per_device(token_ids, routes, gate_weights, embed_table, w_gate, w_up, w_down):
    vocab_rows, width_cols = embed_table.shape
    tokens, top_count = routes.shape
    experts = lax.axis_size("expert")
    group_size = lax.axis_size(("pipe", "vocab"))
    capacity = group_size * (3 * tokens * top_count // (2 * experts * group_size))
    row_base = lax.axis_index(("pipe", "vocab")) * vocab_rows
    local_ids = token_ids - row_base
    in_shard = (local_ids >= 0) & (local_ids < vocab_rows)
    lookup_rows = jnp.take(embed_table, jnp.clip(local_ids, 0, vocab_rows - 1), axis=0)
    lookup_rows = jnp.where(in_shard[:, None], lookup_rows.astype(jnp.float32), 0.0)
    embedded = lax.psum(lookup_rows.astype(jnp.bfloat16), ("pipe", "vocab"))
    flat_routes = routes.reshape(-1)
    one_hot = (flat_routes[:, None] == jnp.arange(experts, dtype=jnp.int32)[None, :]).astype(
        jnp.int32
    )
    slot_index = jnp.sum((jnp.cumsum(one_hot, axis=0) - one_hot) * one_hot, axis=1)
    slot_dest = flat_routes * capacity + slot_index
    repeated = jnp.repeat(embedded, top_count, axis=0)
    buffer = jnp.zeros((experts * capacity, width_cols), jnp.bfloat16).at[slot_dest].set(repeated)
    buffer = buffer.reshape(experts, capacity, width_cols)
    flat_rows = lax.all_to_all(buffer, "expert", split_axis=0, concat_axis=2, tiled=True)[0]
    gate_proj = jnp.dot(flat_rows, w_gate[0], preferred_element_type=jnp.float32)
    up_proj = jnp.dot(flat_rows, w_up[0], preferred_element_type=jnp.float32)
    hidden = (jax.nn.silu(gate_proj) * up_proj).astype(jnp.bfloat16)
    partial_value = jnp.dot(hidden, w_down[0], preferred_element_type=jnp.float32)[None]
    shared = lax.psum_scatter(
        partial_value.astype(jnp.bfloat16), ("pipe", "vocab"), scatter_dimension=1, tiled=True
    ).astype(jnp.float32)
    shared = lax.all_to_all(
        shared.astype(jnp.bfloat16), "expert", split_axis=2, concat_axis=0, tiled=True
    ).astype(shared.dtype)
    returned = lax.all_gather(
        shared.astype(jnp.bfloat16), ("pipe", "vocab"), axis=1, tiled=True
    ).astype(shared.dtype)
    picked = returned.reshape(experts * capacity, width_cols)[slot_dest].reshape(
        tokens, top_count, width_cols
    )
    moe_out = jnp.sum(picked * gate_weights[:, :, None], axis=1)
    residual = (embedded.astype(jnp.float32) + moe_out).astype(jnp.bfloat16)
    return lax.psum_scatter(
        lax.dot_general(
            residual, embed_table, (((1,), (1,)), ((), ())), preferred_element_type=jnp.float32
        ).astype(jnp.bfloat16),
        "expert",
        scatter_dimension=0,
        tiled=True,
    )


def solution(mesh):
    return jax.shard_map(
        per_device,
        mesh=mesh,
        in_specs=(
            P(),
            P(),
            P(),
            P(("pipe", "vocab"), "expert"),
            P("expert", None, ("pipe", "vocab")),
            P("expert", None, ("pipe", "vocab")),
            P("expert", ("pipe", "vocab"), None),
        ),
        out_specs=P("expert", ("pipe", "vocab")),
        check_vma=False,
    )
```

profile of v0, /device:TPU:9, one launch (start us, length us, event | category | flops | bytes accessed | tf_op | source)
XLA Modules:
  0.0 426.0 jit_solution(8567750402209135640)
XLA Ops:
  7.2 14.9 %gather_fusion = bf16[192,1792]{1,0:T(8,128)(2,1)S(1)} fusion(bf16[8192,1792]{1,0:T(8,128)(2,1)} %param.10, s32[1024]{0:T(1024)S(1)} %pad_clamp_fusion.1), kind=kCustom, calls=%fused_computation | custom fusion | bytes 1377024 | tf_op jit(solution)/shard_map/jit(_take)/gather | solution.py:16
  25.9 53.5 %all-reduce.4.cloned.1.call-done = bf16[192,1792]{1,0:T(8,128)(2,1)} async-done(((bf16[192,1792]{1,0:T(8,128)(2,1)}), bf16[192,1792]{1,0:T(8,128)(2,1)}) %all-reduce.4.cloned.1.call-update) | async-done | bytes 688144 | tf_op jit(solution)/shard_map/psum | solution.py:18
  79.3 1.8 broadcast_in_dim.42
  81.7 3.3 scatter_custom_fusion
  85.0 49.3 %all_to_all.33 = bf16[4,144,1792]{2,1,0:T(8,128)(2,1)S(1)} all-to-all(bf16[4,144,1792]{2,1,0:T(8,128)(2,1)S(1)} %bitcast.66), channel_id=1, replica_groups=mesh['pipe'=4,'vocab'=2,'expert'=4] {'expert'}, dimensions={0} | all-to-all | bytes 4128768 | tf_op jit(solution)/shard_map/all_to_all | solution.py:28
  138.3 6.9 %fusion.1 = bf16[1,144,7168]{2,1,0:T(8,128)(2,1)} fusion(bf16[1,256,7168]{2,1,0:T(8,128)(2,1)} %param.13, bf16[144,7168]{1,0:T(8,128)(2,1)S(1)} %bitcast.63, bf16[1,7168,256]{2,1,0:T(8,128)(2,1)} %param.12, f32[144,256]{1,0:T(8,128)S(1)} %fusion.5), kind=kOutput, calls=%fused_computation.5 | convolution fusion | flops 1058217984 | bytes 11616256 | tf_op jit(solution)/shard_map/dot_general | solution.py:32
  145.1 59.6 %fusion = bf16[24,7168]{1,0:T(8,128)(2,1)S(1)} fusion(bf16[1,144,7168]{2,1,0:T(8,128)(2,1)} %fusion.1), kind=kCustom, calls=%all-reduce-scatter | all-reduce-scatter fusion | flops 1376257 | bytes 2408960
  204.8 1.9 collective-permute-start
  206.8 4.0 collective-permute-start.1
  212.1 5.7 %collective-permute-done.1 = bf16[18,7168]{1,0:T(8,128)(2,1)S(1)} collective-permute-done((bf16[18,7168]{1,0:T(8,128)(2,1)S(1)}, bf16[18,7168]{1,0:T(8,128)(2,1)S(1)}, u32[]{:S(2)}, u32[]{:S(2)}) %collective-permute-start.1) | collective-permute-done | bytes 258080
  217.7 4.8 %concatenate = bf16[66,7168]{1,0:T(8,128)(2,1)S(1)} concatenate(bf16[18,7168]{1,0:T(8,128)(2,1)S(1)} %collective-permute-done.1, bf16[24,7168]{1,0:T(8,128)(2,1)S(1)} %collective-permute-done, bf16[24,7168]{1,0:T(8,128)(2,1)S(1)} %fusion), dimensions={0} | concatenate | bytes 1892352
  222.7 6.0 %copy.42 = bf16[1,18,7168]{1,0,2:T(2,128)(2,1)} copy(bf16[1,18,7168]{2,1,0:T(8,128)(2,1)S(1)} %dynamic-slice_bitcast_fusion) | data formatting | bytes 516096 | tf_op jit(solution)/shard_map/reduce_scatter | solution.py:33
  229.2 39.8 %reduce.4 = bf16[7168,18]{1,0:T(8,128)(2,1)S(1)} reduce(bf16[7168,1,18]{2,1,0:T(2,128)(2,1)} %bitcast.64, bf16[]{:T(256)} %broadcast.68), dimensions={1}, to_apply=%bitcast.56.reduce_sub_computation | reduce | bytes 516098
  269.0 3.4 reshape.114
  272.4 9.2 %all_to_all.34 = bf16[4,2,16128]{2,1,0:T(2,128)(2,1)S(1)} all-to-all(bf16[4,2,16128]{2,1,0:T(2,128)(2,1)S(1)} %reshape.114), channel_id=1, replica_groups=mesh['pipe'=4,'vocab'=2,'expert'=4] {'expert'}, dimensions={0} | all-to-all | bytes 516096 | tf_op jit(solution)/shard_map/all_to_all | solution.py:36
  281.6 5.2 %reshape.115 = bf16[7168,1,18]{2,1,0:T(2,128)(2,1)} reshape(bf16[4,2,16128]{2,1,0:T(2,128)(2,1)S(1)} %all_to_all.34) | data formatting | bytes 516096
  286.7 7.3 %copy.43 = bf16[1,18,7168]{2,1,0:T(8,128)(2,1)S(1)} copy(bf16[1,18,7168]{1,0,2:T(2,128)(2,1)} %bitcast.65) | data formatting | bytes 516096 | tf_op jit(solution)/shard_map/all_to_all | solution.py:36
  295.3 28.4 %all-gather.3.cloned.1.call-done = bf16[4,1,144,1792]{3,0,1,2:T(4,128)(2,1)} async-done(((bf16[4,1,18,1792]{3,0,1,2:T(4,128)(2,1)}), bf16[4,1,144,1792]{3,0,1,2:T(4,128)(2,1)}) %all-gather.3.cloned.1.call-update) | async-done | bytes 2064400 | tf_op jit(solution)/shard_map/all_gather | solution.py:39
  325.4 2.4 bitcast_convert_fusion
  327.8 6.1 %gather_fusion.1 = f32[384,1792]{1,0:T(8,128)S(1)} fusion(f32[576,1792]{1,0:T(8,128)} %bitcast_convert_fusion, s32[1024]{0:T(1024)S(1)} %pad_clamp_fusion), kind=kCustom, calls=%fused_computation.1 | custom fusion | bytes 5506560 | tf_op jit(solution)/shard_map/gather | solution.py:42
  333.9 2.8 reshape.75
  336.7 5.9 %multiply_reduce_fusion = f32[192,1792]{1,0:T(8,128)S(1)} fusion(f32[192,2,1792]{2,1,0:T(2,128)} %reshape.75, f32[192,2]{1,0:T(8,128)S(1)} %copy.46), kind=kLoop, calls=%fused_computation.11 | loop fusion | flops 1032192 | bytes 4130304 | tf_op jit(solution)/shard_map/reduce_sum | solution.py:45
  342.6 17.4 %convolution_convert_fusion = bf16[192,8192]{1,0:T(8,128)(2,1)} fusion(bf16[8192,1792]{1,0:T(8,128)(2,1)} %param.10, f32[192,1792]{1,0:T(8,128)S(1)} %multiply_reduce_fusion, bf16[192,1792]{1,0:T(8,128)(2,1)S(1)} %copy-done.1), kind=kOutput, calls=%fused_computation.3 | convolution fusion | flops 5639749632 | bytes 34570240 | tf_op jit(solution)/shard_map/dot_general | solution.py:48
  360.0 59.5 %reduce-scatter.5.cloned.1.call-done = bf16[48,8192]{1,0:T(8,128)(2,1)} async-done(((bf16[192,8192]{1,0:T(8,128)(2,1)}), bf16[48,8192]{1,0:T(8,128)(2,1)}) %reduce-scatter.5.cloned.1.call-update) | async-done | bytes 786448 | tf_op jit(solution)/shard_map/reduce_scatter | solution.py:47
  (45 shorter events, 13.1 us)
Async XLA Ops:
  6.5 72.8 %all-reduce.4.cloned.1.call-start = ((), (), s32[]{:S(2)}) async-start(), calls=%async_computation.3 | async-start | bytes 1376256 | tf_op jit(solution)/shard_map/psum | solution.py:18
  22.1 1.3 copy-start.2
  23.3 300.3 %all-gather.3.cloned.1.call-start = ((), (), s32[]{:S(2)}) async-start(), calls=%async_computation.5 | async-start | bytes 2322432 | tf_op jit(solution)/shard_map/all_gather | solution.py:39
  135.4 2.0 copy-start
  145.1 65.7 %copy-start.4 = (u32[32]{0:T(128)S(1)}, u32[32]{0:T(128)}, u32[]{:S(2)}) copy-start(u32[32]{0:T(128)} %constant.54) | copy-start | bytes 388
  204.8 13.0 %collective-permute-start = (bf16[24,7168]{1,0:T(8,128)(2,1)S(1)}, bf16[24,7168]{1,0:T(8,128)(2,1)S(1)}, u32[]{:S(2)}, u32[]{:S(2)}) collective-permute-start(bf16[24,7168]{1,0:T(8,128)(2,1)S(1)} %fusion), channel_id=1, source_target_pairs={{0,4},{4,8},{8,12},{12,16},{16,20},{20,24},{24,28},{1,5},{5,9},{9,... | collective-permute-start | bytes 1032200
  206.8 10.9 %collective-permute-start.1 = (bf16[18,7168]{1,0:T(8,128)(2,1)S(1)}, bf16[18,7168]{1,0:T(8,128)(2,1)S(1)}, u32[]{:S(2)}, u32[]{:S(2)}) collective-permute-start(bf16[18,7168]{1,0:T(8,128)(2,1)S(1)} %slice.13), channel_id=1, source_target_pairs={{0,8},{4,12},{8,16},{12,20},{16,24},{20,28},{1,9},{5,13},{9,17},{1... | collective-permute-start | bytes 774152
  286.7 8.4 %copy-start.3 = (f32[192,2]{0,1:T(2,128)S(1)}, f32[192,2]{0,1:T(2,128)}, u32[]{:S(2)}) copy-start(f32[192,2]{0,1:T(2,128)} %param.9) | copy-start | bytes 4612
  294.9 124.6 %reduce-scatter.5.cloned.1.call-start = ((), (), s32[]{:S(2)}) async-start(), calls=%async_computation.4 | async-start | bytes 3932160 | tf_op jit(solution)/shard_map/reduce_scatter | solution.py:47
  336.7 5.9 %copy-start.1 = (bf16[192,1792]{1,0:T(8,128)(2,1)S(1)}, bf16[192,1792]{1,0:T(8,128)(2,1)}, u32[]{:S(2)}) copy-start(bf16[192,1792]{1,0:T(8,128)(2,1)} %all-reduce.4.cloned.1.call-done) | copy-start | bytes 2064388
Sparse Core Ops, SparseCore 0:
  23.5 55.8 all-reduce.3
  295.0 28.6 all-gather.2
  360.1 59.3 reduce-scatter.4
where the time goes:
time: 429 us; the launch traced here: 426 us
  waiting for transfers between devices  147 us (34%)
  blocking collectives  118 us (28%)
  local copies, waits for them, and re-layouts  64 us (15%)
  other arithmetic  51.5 us (12%)
  matrix products  25 us (6%)
  between operations  14 us (3%)
  starting transfers between devices  6.25 us (1%)
    unnamed x1, blocking collectives  59.6 us
    reduce_scatter x1, waiting for transfers between devices, per_device(): lax.psum_scatter(lax.dot_general(residual, embed_table, (((1,), (1,)), ((...  59.5 us
    psum x1, waiting for transfers between devices, per_device(): embedded = lax.psum(lookup_rows.astype(jnp.bfloat16), ('pipe', 'vocab'))  53.5 us
    all_to_all x1, blocking collectives, per_device(): lax.all_to_all(buffer, 'expert', split_axis=0, concat_axis=2, tiled=True)[0]  49.3 us
    unnamed x2, other arithmetic  39.8 us
    all_gather x1, waiting for transfers between devices, per_device(): lax.all_gather(shared.astype(jnp.bfloat16), ('pipe', 'vocab'), axis=1, ti...  28.4 us
    dot_general x1, matrix products, per_device(): lax.dot_general(residual, embed_table, (((1,), (1,)), ((), ())), preferre...  17.4 us
    unnamed x20, local copies, waits for them, and re-layouts  16.9 us
  transfers between devices with their start and end apart: 5, of which 4 were waited for; matrix products, arithmetic and copies ran while one was open for 1% of the time, Pallas kernels for 0%

commit v1 on v0

v1 whole, which is shorter than its diff:
```python
import functools

import jax
import jax.numpy as jnp
from jax import lax
from jax.experimental import pallas as pl
from jax.experimental.pallas import tpu as pltpu
from jax.sharding import PartitionSpec as P

MESH = pl.DeviceIdType.MESH
GROUP = ("pipe", "vocab")


def peer_coords(axes, sizes, index):
    coords = {}
    for axis, size in reversed(list(zip(axes, sizes))):
        coords[axis] = index % size
        index = index // size
    return coords


def exchange_kernel(axes, sizes, reduce, x_ref, o_ref, *scratch):
    n = 1
    for size in sizes:
        n *= size
    me = 0
    for axis, size in zip(axes, sizes):
        me = me * size + lax.axis_index(axis)
    if reduce:
        land, send_sem, recv_sem = scratch
    else:
        land = o_ref
        send_sem, recv_sem, local_sem = scratch
    barrier = pltpu.get_barrier_semaphore()
    for k in range(1, n):
        where = peer_coords(axes, sizes, (me + k) % n)
        pl.semaphore_signal(barrier, inc=1, device_id=where, device_id_type=MESH)
    pl.semaphore_wait(barrier, n - 1)
    copies = []
    for k in range(1, n):
        peer = (me + k) % n
        copy = pltpu.make_async_remote_copy(
            src_ref=x_ref.at[peer] if reduce else x_ref,
            dst_ref=land.at[k - 1] if reduce else land.at[me],
            send_sem=send_sem.at[k - 1],
            recv_sem=recv_sem.at[k - 1],
            device_id=peer_coords(axes, sizes, peer),
            device_id_type=MESH,
        )
        copy.start()
        copies.append(copy)
    if not reduce:
        own = pltpu.make_async_copy(x_ref, land.at[me], local_sem)
        own.start()
        own.wait()
    for copy in copies:
        copy.wait()
    if reduce:
        columns = o_ref.shape[-1]
        tile = next((t for t in (512, 256, 128) if columns % t == 0), columns)

        @pl.loop(0, columns // tile)
        def _(step):
            cols = pl.ds(pl.multiple_of(step * tile, tile), tile)
            total = x_ref[me, :, cols].astype(jnp.float32)
            for k in range(n - 1):
                total = total + land[k, :, cols].astype(jnp.float32)
            o_ref[:, cols] = total.astype(o_ref.dtype)


def exchange(x, axes, reduce, collective_id, out_dtype=None):
    sizes = tuple(lax.axis_size(axis) for axis in axes)
    n = 1
    for size in sizes:
        n *= size
    block = x.shape[1:] if reduce else x.shape
    out = jax.ShapeDtypeStruct(block if reduce else (n,) + block, out_dtype or x.dtype)
    sems = [pltpu.SemaphoreType.DMA((n - 1,)), pltpu.SemaphoreType.DMA((n - 1,))]
    if reduce:
        scratch = [pltpu.VMEM((n - 1,) + block, x.dtype)] + sems
    else:
        scratch = sems + [pltpu.SemaphoreType.DMA]
    return pl.pallas_call(
        functools.partial(exchange_kernel, axes, sizes, reduce),
        out_shape=out,
        in_specs=[pl.BlockSpec(memory_space=pltpu.VMEM)],
        out_specs=pl.BlockSpec(memory_space=pltpu.VMEM),
        scratch_shapes=scratch,
        compiler_params=pltpu.CompilerParams(collective_id=collective_id, has_side_effects=True),
    )(x)


def per_device(token_ids, routes, gate_weights, embed_table, w_gate, w_up, w_down):
    vocab_rows, width_cols = embed_table.shape
    tokens = routes.shape[0]
    experts = lax.axis_size("expert")
    group = lax.axis_size(GROUP)
    width = experts * width_cols
    part = tokens // group
    row_base = lax.axis_index(GROUP) * vocab_rows
    local_ids = token_ids - row_base
    in_shard = (local_ids >= 0) & (local_ids < vocab_rows)
    rows = embed_table.at[jnp.clip(local_ids, 0, vocab_rows - 1)].get(mode="promise_in_bounds")
    rows = jnp.where(in_shard[:, None], rows, jnp.zeros_like(rows))
    own = exchange(rows.reshape(group, part, width_cols), GROUP, True, 0)
    wide = exchange(own, ("expert",), False, 1)
    wide = wide.transpose(1, 0, 2).reshape(part, width)
    embedded = exchange(wide, GROUP, False, 2).reshape(tokens, width)
    gate_proj = jnp.dot(embedded, w_gate[0], preferred_element_type=jnp.float32)
    up_proj = jnp.dot(embedded, w_up[0], preferred_element_type=jnp.float32)
    hidden = (jax.nn.silu(gate_proj) * up_proj).astype(jnp.bfloat16)
    share = jnp.sum(
        jnp.where(routes == lax.axis_index("expert"), gate_weights, 0.0), axis=1, keepdims=True
    )
    partial_out = jnp.dot(hidden, w_down[0], preferred_element_type=jnp.float32) * share
    partial_out = partial_out.astype(jnp.bfloat16).reshape(group, part, width)
    summed = exchange(partial_out, GROUP, True, 3)
    summed = summed.reshape(part, experts, width_cols).transpose(1, 0, 2)
    moe_out = exchange(summed, ("expert",), True, 4, jnp.float32)
    residual = (own.astype(jnp.float32) + moe_out).astype(jnp.bfloat16)
    residual = exchange(residual, GROUP, False, 5).reshape(tokens, width_cols)
    logits = lax.dot_general(
        residual, embed_table, (((1,), (1,)), ((), ())), preferred_element_type=jnp.float32
    ).astype(jnp.bfloat16)
    return exchange(logits.reshape(experts, tokens // experts, vocab_rows), ("expert",), True, 6)


def solution(mesh):
    return jax.shard_map(
        per_device,
        mesh=mesh,
        in_specs=(
            P(),
            P(),
            P(),
            P(GROUP, "expert"),
            P("expert", None, GROUP),
            P("expert", None, GROUP),
            P("expert", GROUP, None),
        ),
        out_specs=P("expert", GROUP),
        check_vma=False,
    )
```

time: 429 us -> 251 us (0.59)
  Pallas kernels: 0 us -> 198 us
  waiting for transfers between devices: 147 us -> 0 us
  blocking collectives: 118 us -> 0 us
  other arithmetic: 51.5 us -> 4.63 us
  local copies, waits for them, and re-layouts: 64 us -> 20.5 us
  between operations: 14 us -> 0.1 us
  starting transfers between devices: 6.25 us -> 0 us
    pallas_call x0 -> x7, Pallas kernels: none -> 198 us  [exchange(): pl.pallas_call(functools.partial(exchange_kernel, axes, sizes, reduce), o...]
    unnamed x1 -> x0, blocking collectives: 59.6 us -> none
    reduce_scatter x1 -> x0, waiting for transfers between devices: 59.5 us -> none  [per_device(): lax.psum_scatter(lax.dot_general(residual, embed_table, (((1,), (1,)), ((...]
    all_to_all x2 -> x0, blocking collectives: 58.5 us -> none  [the longest x1 49.3 us: per_device(): lax.all_to_all(buffer, 'expert', split_axis=0, concat_axis=2, tiled=True)[0]]
    psum x1 -> x0, waiting for transfers between devices: 53.5 us -> none  [per_device(): embedded = lax.psum(lookup_rows.astype(jnp.bfloat16), ('pipe', 'vocab'))]
    unnamed x2 -> x0, other arithmetic: 39.8 us -> none
    all_gather x1 -> x0, waiting for transfers between devices: 28.4 us -> none  [per_device(): lax.all_gather(shared.astype(jnp.bfloat16), ('pipe', 'vocab'), axis=1, ti...]
    unnamed x20 -> x5, local copies, waits for them, and re-layouts: 16.9 us -> 2.07 us
  transfers between devices with their start and end apart: 5 -> 0, of which waited for: 4 -> 0; matrix products, arithmetic and copies ran while one was open for 1% -> 0% of each run, Pallas kernels for 0% -> 0%
where the time goes in v1:
time: 251 us
  Pallas kernels  198 us (79%)
  matrix products  27.5 us (11%)
  local copies, waits for them, and re-layouts  20.5 us (8%)
  other arithmetic  4.63 us (2%)
    pallas_call x7, Pallas kernels, exchange(): pl.pallas_call(functools.partial(exchange_kernel, axes, sizes, reduce), o...  198 us
    dot_general x1, matrix products, per_device(): lax.dot_general(residual, embed_table, (((1,), (1,)), ((), ())), preferre...  15.8 us
    gather x1, local copies, waits for them, and re-layouts, per_device(): embed_table.at[jnp.clip(local_ids, 0, vocab_rows - 1)]  14.9 us
    dot_general x1, matrix products, per_device(): jnp.dot(hidden, w_down[0], preferred_element_type=jnp.float32) * share  7.79 us

profile of v1, /device:TPU:9, one launch (start us, length us, event | category | flops | bytes accessed | tf_op | source)
XLA Modules:
  0.0 250.7 jit_solution(13765104149929191110)
XLA Ops:
  0.0 0.7 fusion.20
  0.7 0.7 compare_and_fusion
  1.4 0.7 compare_select_fusion.1
  2.1 0.1 broadcast_in_dim.22
  2.2 14.9 %gather_fusion = bf16[192,1792]{1,0:T(8,128)(2,1)S(1)} fusion(bf16[8192,1792]{1,0:T(8,128)(2,1)} %param.10, s32[1024]{0:T(1024)S(1)} %pad_clamp_fusion), kind=kCustom, calls=%fused_computation | custom fusion | bytes 1377024 | tf_op jit(solution)/shard_map/gather | solution.py:103
  17.1 1.0 broadcast_select_fusion.x_ref
  18.0 13.6 %shard_map.73.x_ref = bf16[24,1792]{1,0:T(8,128)(2,1)} custom-call(bf16[8,24,1792]{2,1,0:T(8,128)(2,1)} %broadcast_select_fusion.x_ref), custom_call_target="tpu_custom_call" | custom-call | tf_op jit(solution)/shard_map/pallas_call | solution.py:83
  31.6 12.7 %shard_map.74 = bf16[4,24,1792]{2,1,0:T(8,128)(2,1)} custom-call(bf16[24,1792]{1,0:T(8,128)(2,1)} %shard_map.73.x_ref), custom_call_target="tpu_custom_call" | custom-call | tf_op jit(solution)/shard_map/pallas_call | solution.py:83
  44.3 1.7 copy.12
  46.1 35.9 %shard_map.75 = bf16[8,24,7168]{2,1,0:T(8,128)(2,1)} custom-call(bf16[24,7168]{1,0:T(8,128)(2,1)} %bitcast.39), custom_call_target="tpu_custom_call" | custom-call | tf_op jit(solution)/shard_map/pallas_call | solution.py:83
  82.0 0.0 copy-start
  82.0 3.9 %fusion.4 = f32[192,256]{1,0:T(8,128)S(1)} fusion(bf16[192,7168]{1,0:T(8,128)(2,1)} %bitcast.34, bf16[1,7168,256]{2,1,0:T(8,128)(2,1)} %param.11), kind=kOutput, calls=%fused_computation.7 | convolution fusion | flops 704643072 | bytes 6619136 | tf_op jit(solution)/shard_map/dot_general | solution.py:109
  85.9 0.0 copy-done
  85.9 7.8 %fusion = bf16[192,7168]{1,0:T(8,128)(2,1)} fusion(bf16[1,256,7168]{2,1,0:T(8,128)(2,1)} %param.13, f32[192]{0:T(256)S(1)} %fusion.20, bf16[192,7168]{1,0:T(8,128)(2,1)S(1)} %bitcast.35, bf16[1,7168,256]{2,1,0:T(8,128)(2,1)} %param.12, f32[192,256]{1,0:T(8,128)S(1)} %fusion.4), kind=kOutput, calls=%fused_computation.3 | convolution fusion | flops 1412333568 | bytes 13042432 | tf_op jit(solution)/shard_map/dot_general | solution.py:115
  93.7 0.0 copy-start.1
  93.7 35.9 %shard_map.76 = bf16[24,7168]{1,0:T(8,128)(2,1)} custom-call(bf16[8,24,7168]{2,1,0:T(8,128)(2,1)} %bitcast.36), custom_call_target="tpu_custom_call" | custom-call | tf_op jit(solution)/shard_map/pallas_call | solution.py:83
  129.6 1.7 copy.14
  131.3 12.7 %shard_map.77 = f32[24,1792]{1,0:T(8,128)} custom-call(bf16[4,24,1792]{2,1,0:T(8,128)(2,1)} %bitcast.41), custom_call_target="tpu_custom_call" | custom-call | tf_op jit(solution)/shard_map/pallas_call | solution.py:83
  144.0 0.0 copy-done.1
  144.0 1.6 add_convert_fusion.x_ref
  145.6 13.0 %shard_map.78 = bf16[8,24,1792]{2,1,0:T(8,128)(2,1)} custom-call(bf16[24,1792]{1,0:T(8,128)(2,1)} %add_convert_fusion.x_ref), custom_call_target="tpu_custom_call" | custom-call | tf_op jit(solution)/shard_map/pallas_call | solution.py:83
  158.5 15.8 %convolution_convert_fusion = bf16[192,8192]{1,0:T(8,128)(2,1)} fusion(bf16[192,1792]{1,0:T(8,128)(2,1)} %bitcast.43, bf16[8192,1792]{1,0:T(8,128)(2,1)} %param.10), kind=kOutput, calls=%fused_computation.1 | convolution fusion | flops 5638717440 | bytes 33193984 | tf_op jit(solution)/shard_map/dot_general | solution.py:122
  174.4 74.3 %shard_map.79 = bf16[48,8192]{1,0:T(8,128)(2,1)} custom-call(bf16[4,48,8192]{2,1,0:T(8,128)(2,1)} %bitcast.37), custom_call_target="tpu_custom_call" | custom-call | tf_op jit(solution)/shard_map/pallas_call | solution.py:83
  248.6 2.1 copy.16
  (1 shorter events, 0.0 us)
Async XLA Ops:
  82.0 3.9 %copy-start = (bf16[8,24,7168]{2,1,0:T(8,128)(2,1)S(1)}, bf16[8,24,7168]{2,1,0:T(8,128)(2,1)}, u32[]{:S(2)}) copy-start(bf16[8,24,7168]{2,1,0:T(8,128)(2,1)} %shard_map.75) | copy-start | bytes 8257540
  93.7 50.3 %copy-start.1 = (bf16[24,1792]{1,0:T(8,128)(2,1)S(1)}, bf16[24,1792]{1,0:T(8,128)(2,1)}, u32[]{:S(2)}) copy-start(bf16[24,1792]{1,0:T(8,128)(2,1)} %shard_map.73.x_ref) | copy-start | bytes 258052

commit v2 on v1

--- a/solution.py
+++ b/solution.py
@@ -90,6 +90,198 @@
     )(x)
 
 
+def core_pair_kernel(sizes, reduce, x_ref, o_ref, *scratch):
+    pipes, vocabs = sizes
+    p, v = lax.axis_index("pipe"), lax.axis_index("vocab")
+    core, me = p % 2, p * vocabs + v
+    chips = pipes * vocabs // 2
+    chip = (p // 2) * vocabs + v
+    other = {"pipe": p + 1 - 2 * core, "vocab": v}
+
+    def of_chip(index, on):
+        pipe = (index // vocabs) * 2 + on
+        return {"pipe": pipe, "vocab": index % vocabs}, pipe * vocabs + index % vocabs
+
+    def send(src, dst, sems, at, where):
+        copy = pltpu.make_async_remote_copy(
+            src_ref=src, dst_ref=dst, send_sem=sems.at[0, at], recv_sem=sems.at[1, at],
+            device_id=where, device_id_type=MESH,
+        )
+        copy.start()
+        return copy
+
+    barrier = pltpu.get_barrier_semaphore()
+    pl.semaphore_signal(barrier, inc=1, device_id=other, device_id_type=MESH)
+    for k in range(1, chips):
+        where, _ = of_chip((chip + k) % chips, core)
+        pl.semaphore_signal(barrier, inc=1, device_id=where, device_id_type=MESH)
+    pl.semaphore_wait(barrier, chips)
+    if not reduce:
+        far, near, local_sem = scratch
+        outgoing = []
+        for k in range(1, chips):
+            where, _ = of_chip((chip + k) % chips, core)
+            outgoing.append(send(x_ref, o_ref.at[me], far, k, where))
+        passed = [send(x_ref, o_ref.at[me], near, 0, other)]
+        own = pltpu.make_async_copy(x_ref, o_ref.at[me], local_sem)
+        own.start()
+        for k in range(1, chips):
+            outgoing[k - 1].wait_recv()
+            _, source = of_chip((chip + chips - k) % chips, core)
+            passed.append(send(o_ref.at[source], o_ref.at[source], near, k, other))
+        own.wait()
+        for copy in outgoing:
+            copy.wait_send()
+        for copy in passed:
+            copy.wait()
+        return
+    paired, merged, land, far, near = scratch
+    columns = o_ref.shape[-1]
+    tile = next((t for t in (512, 256, 128) if columns % t == 0), columns)
+
+    def each_tile(body):
+        @pl.loop(0, columns // tile)
+        def _(step):
+            body(pl.ds(pl.multiple_of(step * tile, tile), tile))
+
+    given = []
+    order = list(range(1, chips)) + [0]
+    for k in order:
+        _, index = of_chip((chip + k) % chips, 1 - core)
+        given.append(send(x_ref.at[index], paired.at[k], near, k, other))
+    outgoing, ready = [], None
+    for copy, k in zip(given, order):
+        copy.wait_recv()
+        where, index = of_chip((chip + k) % chips, core)
+
+        def merge(cols):
+            total = x_ref[index, :, cols].astype(jnp.float32)
+            total = total + paired[k, :, cols].astype(jnp.float32)
+            merged[k, :, cols] = total.astype(merged.dtype)
+
+        if k:
+            each_tile(merge)
+        if ready is not None:
+            at, to = ready
+            outgoing.append(send(merged.at[at], land.at[at], far, at, to))
+        ready = (k, where)
+    for copy in given:
+        copy.wait_send()
+    for copy in outgoing:
+        copy.wait()
+
+    def finish(cols):
+        total = x_ref[me, :, cols].astype(jnp.float32) + paired[0, :, cols].astype(jnp.float32)
+        for k in range(1, chips):
+            total = total + land[k, :, cols].astype(jnp.float32)
+        o_ref[:, cols] = total.astype(o_ref.dtype)
+
+    each_tile(finish)
+
+
+def core_pair_exchange(x, reduce, collective_id):
+    sizes = tuple(lax.axis_size(axis) for axis in GROUP)
+    n = sizes[0] * sizes[1]
+    chips = n // 2
+    block = x.shape[1:] if reduce else x.shape
+    pair_sems = [pltpu.SemaphoreType.DMA((2, chips)), pltpu.SemaphoreType.DMA((2, chips))]
+    if reduce:
+        scratch = [pltpu.VMEM((chips,) + block, x.dtype)] * 3 + pair_sems
+    else:
+        scratch = pair_sems + [pltpu.SemaphoreType.DMA]
+    return pl.pallas_call(
+        functools.partial(core_pair_kernel, sizes, reduce),
+        out_shape=jax.ShapeDtypeStruct(block if reduce else (n,) + block, x.dtype),
+        in_specs=[pl.BlockSpec(memory_space=pltpu.VMEM)],
+        out_specs=pl.BlockSpec(memory_space=pltpu.VMEM),
+        scratch_shapes=scratch,
+        compiler_params=pltpu.CompilerParams(collective_id=collective_id, has_side_effects=True),
+    )(x)
+
+
+def logits_kernel(n, steps, x_ref, table_ref, o_ref, held, land, send_sem, recv_sem):
+    step = pl.program_id(0)
+    me = lax.axis_index("expert")
+    part, tile = held.shape[1], table_ref.shape[0]
+
+    def sends(at):
+        cols = pl.ds(pl.multiple_of(at * tile, tile), tile)
+        return [
+            pltpu.make_async_remote_copy(
+                src_ref=held.at[(me + k) % n, :, cols],
+                dst_ref=land.at[k - 1, :, cols],
+                send_sem=send_sem.at[k - 1, at],
+                recv_sem=recv_sem.at[k - 1, at],
+                device_id={"expert": (me + k) % n},
+                device_id_type=MESH,
+            )
+            for k in range(1, n)
+        ]
+
+    @pl.when(step == 0)
+    def _():
+        barrier = pltpu.get_barrier_semaphore()
+        for k in range(1, n):
+            pl.semaphore_signal(
+                barrier, inc=1, device_id={"expert": (me + k) % n}, device_id_type=MESH
+            )
+        pl.semaphore_wait(barrier, n - 1)
+
+    @pl.when(step > 0)
+    def _():
+        for copy in sends(step - 1):
+            copy.start()
+
+    block = lax.dot_general(
+        x_ref[...], table_ref[...], (((1,), (1,)), ((), ())), preferred_element_type=jnp.float32
+    ).astype(held.dtype)
+    here = pl.ds(pl.multiple_of(step * tile, tile), tile)
+    for i in range(n):
+        held[i, :, here] = block[i * part : (i + 1) * part]
+
+    @pl.when(step == steps - 1)
+    def _():
+        for copy in sends(steps - 1):
+            copy.start()
+
+        @pl.loop(0, steps)
+        def _(at):
+            for copy in sends(at):
+                copy.wait()
+            cols = pl.ds(pl.multiple_of(at * tile, tile), tile)
+            total = held[me, :, cols].astype(jnp.float32)
+            for k in range(n - 1):
+                total = total + land[k, :, cols].astype(jnp.float32)
+            o_ref[:, cols] = total.astype(o_ref.dtype)
+
+
+def logits_sum(residual, table, collective_id):
+    n = lax.axis_size("expert")
+    (tokens, width), rows = residual.shape, table.shape[0]
+    part, tile = tokens // n, 512
+    steps = rows // tile
+    return pl.pallas_call(
+        functools.partial(logits_kernel, n, steps),
+        grid=(steps,),
+        out_shape=jax.ShapeDtypeStruct((part, rows), residual.dtype),
+        in_specs=[
+            pl.BlockSpec((tokens, width), lambda i: (0, 0)),
+            pl.BlockSpec((tile, width), lambda i: (i, 0)),
+        ],
+        out_specs=pl.BlockSpec((part, rows), lambda i: (0, 0)),
+        scratch_shapes=[
+            pltpu.VMEM((n, part, rows), residual.dtype),
+            pltpu.VMEM((n - 1, part, rows), residual.dtype),
+            pltpu.SemaphoreType.DMA((n - 1, steps)),
+            pltpu.SemaphoreType.DMA((n - 1, steps)),
+        ],
+        compiler_params=pltpu.CompilerParams(
+            collective_id=collective_id, has_side_effects=True,
+            dimension_semantics=("arbitrary",),
+        ),
+    )(residual, table)
+
+
 def per_device(token_ids, routes, gate_weights, embed_table, w_gate, w_up, w_down):
     vocab_rows, width_cols = embed_table.shape
     tokens = routes.shape[0]
@@ -105,7 +297,7 @@
     own = exchange(rows.reshape(group, part, width_cols), GROUP, True, 0)
     wide = exchange(own, ("expert",), False, 1)
     wide = wide.transpose(1, 0, 2).reshape(part, width)
-    embedded = exchange(wide, GROUP, False, 2).reshape(tokens, width)
+    embedded = core_pair_exchange(wide, False, 2).reshape(tokens, width)
     gate_proj = jnp.dot(embedded, w_gate[0], preferred_element_type=jnp.float32)
     up_proj = jnp.dot(embedded, w_up[0], preferred_element_type=jnp.float32)
     hidden = (jax.nn.silu(gate_proj) * up_proj).astype(jnp.bfloat16)
@@ -114,15 +306,12 @@
     )
     partial_out = jnp.dot(hidden, w_down[0], preferred_element_type=jnp.float32) * share
     partial_out = partial_out.astype(jnp.bfloat16).reshape(group, part, width)
-    summed = exchange(partial_out, GROUP, True, 3)
+    summed = core_pair_exchange(partial_out, True, 3)
     summed = summed.reshape(part, experts, width_cols).transpose(1, 0, 2)
     moe_out = exchange(summed, ("expert",), True, 4, jnp.float32)
     residual = (own.astype(jnp.float32) + moe_out).astype(jnp.bfloat16)
     residual = exchange(residual, GROUP, False, 5).reshape(tokens, width_cols)
-    logits = lax.dot_general(
-        residual, embed_table, (((1,), (1,)), ((), ())), preferred_element_type=jnp.float32
-    ).astype(jnp.bfloat16)
-    return exchange(logits.reshape(experts, tokens // experts, vocab_rows), ("expert",), True, 6)
+    return logits_sum(residual, embed_table, 6)
 
 
 def solution(mesh):

time: 251 us -> 212 us (0.84)
  Pallas kernels: 198 us -> 173 us
  matrix products: 27.5 us -> 11.7 us
    pallas_call x7 -> x4, Pallas kernels: 198 us -> 51.5 us  [exchange(): pl.pallas_call(functools.partial(exchange_kernel, axes, sizes, reduce), o...]
    pallas_call x0 -> x3, Pallas kernels: none -> 121 us  [the longest x1 74.9 us: logits_sum(): pl.pallas_call(functools.partial(logits_kernel, n, steps), grid=(steps,),...]
    dot_general x1 -> x0, matrix products: 15.8 us -> none  [per_device(): lax.dot_general(residual, embed_table, (((1,), (1,)), ((), ())), preferre...]
where the time goes in v2:
time: 212 us; the launch traced here: 210 us
  Pallas kernels  173 us (82%)
  local copies, waits for them, and re-layouts  20.5 us (10%)
  matrix products  11.7 us (6%)
  other arithmetic  4.63 us (2%)
    pallas_call x1, Pallas kernels, logits_sum(): pl.pallas_call(functools.partial(logits_kernel, n, steps), grid=(steps,),...  74.9 us
    pallas_call x4, Pallas kernels, exchange(): pl.pallas_call(functools.partial(exchange_kernel, axes, sizes, reduce), o...  51.5 us
    pallas_call x2, Pallas kernels, core_pair_exchange(): pl.pallas_call(functools.partial(core_pair_kernel, sizes, reduce), out_sh...  46.4 us
    gather x1, local copies, waits for them, and re-layouts, per_device(): embed_table.at[jnp.clip(local_ids, 0, vocab_rows - 1)]  14.9 us
    dot_general x1, matrix products, per_device(): jnp.dot(hidden, w_down[0], preferred_element_type=jnp.float32) * share  7.79 us

profile of v2, /device:TPU:9, one launch (start us, length us, event | category | flops | bytes accessed | tf_op | source)
XLA Modules:
  0.0 209.7 jit_solution(10999699516463456529)
XLA Ops:
  0.0 0.7 fusion.20
  0.7 0.7 compare_and_fusion
  1.4 0.7 compare_select_fusion.1
  2.1 0.1 broadcast_in_dim.22
  2.2 14.9 %gather_fusion = bf16[192,1792]{1,0:T(8,128)(2,1)S(1)} fusion(bf16[8192,1792]{1,0:T(8,128)(2,1)} %table_ref.1, s32[1024]{0:T(1024)S(1)} %pad_clamp_fusion), kind=kCustom, calls=%fused_computation | custom fusion | bytes 1377024 | tf_op jit(solution)/shard_map/gather | solution.py:295
  17.1 1.0 broadcast_select_fusion.x_ref
  18.0 13.6 %shard_map.73.x_ref = bf16[24,1792]{1,0:T(8,128)(2,1)} custom-call(bf16[8,24,1792]{2,1,0:T(8,128)(2,1)} %broadcast_select_fusion.x_ref), custom_call_target="tpu_custom_call" | custom-call | tf_op jit(solution)/shard_map/pallas_call | solution.py:83
  31.6 12.7 %shard_map.74 = bf16[4,24,1792]{2,1,0:T(8,128)(2,1)} custom-call(bf16[24,1792]{1,0:T(8,128)(2,1)} %shard_map.73.x_ref), custom_call_target="tpu_custom_call" | custom-call | tf_op jit(solution)/shard_map/pallas_call | solution.py:83
  44.3 1.7 copy.12
  46.1 22.8 %shard_map.75 = bf16[8,24,7168]{2,1,0:T(8,128)(2,1)} custom-call(bf16[24,7168]{1,0:T(8,128)(2,1)} %bitcast.36), custom_call_target="tpu_custom_call" | custom-call | tf_op jit(solution)/shard_map/pallas_call | solution.py:192
  68.9 0.0 copy-start
  68.9 3.9 %fusion.4 = f32[192,256]{1,0:T(8,128)S(1)} fusion(bf16[192,7168]{1,0:T(8,128)(2,1)} %bitcast.31, bf16[1,7168,256]{2,1,0:T(8,128)(2,1)} %param.11), kind=kOutput, calls=%fused_computation.6 | convolution fusion | flops 704643072 | bytes 6619136 | tf_op jit(solution)/shard_map/dot_general | solution.py:301
  72.8 0.0 copy-done
  72.8 7.8 %fusion = bf16[192,7168]{1,0:T(8,128)(2,1)} fusion(bf16[1,256,7168]{2,1,0:T(8,128)(2,1)} %param.13, f32[192]{0:T(256)S(1)} %fusion.20, bf16[192,7168]{1,0:T(8,128)(2,1)S(1)} %bitcast.32, bf16[1,7168,256]{2,1,0:T(8,128)(2,1)} %param.12, f32[192,256]{1,0:T(8,128)S(1)} %fusion.4), kind=kOutput, calls=%fused_computation.2 | convolution fusion | flops 1412333568 | bytes 13042432 | tf_op jit(solution)/shard_map/dot_general | solution.py:307
  80.6 0.0 copy-start.1
  80.6 23.5 %shard_map.76 = bf16[24,7168]{1,0:T(8,128)(2,1)} custom-call(bf16[8,24,7168]{2,1,0:T(8,128)(2,1)} %bitcast.33), custom_call_target="tpu_custom_call" | custom-call | tf_op jit(solution)/shard_map/pallas_call | solution.py:192
  104.2 1.7 copy.14
  105.9 12.4 %shard_map.77 = f32[24,1792]{1,0:T(8,128)} custom-call(bf16[4,24,1792]{2,1,0:T(8,128)(2,1)} %bitcast.38), custom_call_target="tpu_custom_call" | custom-call | tf_op jit(solution)/shard_map/pallas_call | solution.py:83
  118.3 0.0 copy-done.1
  118.3 1.6 add_convert_fusion.x_ref
  119.9 12.8 %shard_map.78 = bf16[8,24,1792]{2,1,0:T(8,128)(2,1)} custom-call(bf16[24,1792]{1,0:T(8,128)(2,1)} %add_convert_fusion.x_ref), custom_call_target="tpu_custom_call" | custom-call | tf_op jit(solution)/shard_map/pallas_call | solution.py:83
  132.7 74.9 %shard_map.79 = bf16[48,8192]{1,0:T(8,128)(2,1)} custom-call(bf16[192,1792]{1,0:T(8,128)(2,1)} %bitcast.35, bf16[8192,1792]{1,0:T(8,128)(2,1)} %table_ref.1), custom_call_target="tpu_custom_call" | custom-call | tf_op jit(solution)/shard_map/pallas_call | solution.py:263
  207.6 2.1 copy.16
  (1 shorter events, 0.0 us)
Async XLA Ops:
  68.9 3.9 %copy-start = (bf16[8,24,7168]{2,1,0:T(8,128)(2,1)S(1)}, bf16[8,24,7168]{2,1,0:T(8,128)(2,1)}, u32[]{:S(2)}) copy-start(bf16[8,24,7168]{2,1,0:T(8,128)(2,1)} %shard_map.75) | copy-start | bytes 8257540
  80.6 37.6 %copy-start.1 = (bf16[24,1792]{1,0:T(8,128)(2,1)S(1)}, bf16[24,1792]{1,0:T(8,128)(2,1)}, u32[]{:S(2)}) copy-start(bf16[24,1792]{1,0:T(8,128)(2,1)} %shard_map.73.x_ref) | copy-start | bytes 258052
